TPU v7x, 128 devices: a whole 4x4x4 slice. The times are simulated.
128 devices in a mesh: tp: 4 (over y_hi, core), grp: 32 (over z, x, y_lo).
Axes of the slice: x: 4, y: 4 (y_hi: 2, y_lo: 2; y = y_hi * 2 + y_lo), z: 4, core: 2. Of those that a mesh axis runs over, the one named last changes fastest.
Arguments:
- teacher_state: bfloat16 [8192, 5280], P('grp'), may hold values from -6 to 6
- injection: bfloat16 [8192, 5280], P('grp'), may hold values from -6 to 6
- teacher_up: bfloat16 [5280, 8960], P(None, 'tp'), may hold values from -0.078125 to 0.078125
- teacher_down: bfloat16 [8960, 5280], P('tp', 'grp'), may hold values from -0.0625 to 0.0625
- student_up: bfloat16 [5280, 256], P('grp', 'tp'), may hold values from -0.078125 to 0.078125
- student_down: bfloat16 [256, 5280], P('tp', 'grp'), may hold values from -0.375 to 0.375
- teacher_step: int32 [8], replicated, may hold values from 0 to 1
- student_depth: int32 [8], replicated, may hold values from 1 to 2
Outputs:
- grad_up: float32 [5280, 256], P('grp', 'tp')
- grad_down: float32 [256, 5280], P('tp', 'grp')
All inputs are finite; a program needn't handle non-finite values.
Results may differ from a plain program's by a relative error of at most 0.02.
Values may be sent and summed in bfloat16 or wider, within the bound.
A program may use at most 192 MiB of HBM per device.

v0:
```python
import jax
import jax.numpy as jnp
from jax import lax
from jax.sharding import PartitionSpec as P

LENGTH = 1024
S_ITERS = 2
epsilon = 1e-06
loss_scale = 64.0


def in_order(tiles, dim):
    shape = list(tiles.shape[1:])
    shape[dim] *= tiles.shape[0]
    return jnp.moveaxis(tiles, 0, dim).reshape(shape)


def on_gathered_pieces(value, axis, dim, apply, out_dim):
    size, extent = (lax.axis_size(axis), value.shape[dim])
    count = 2 if extent % 2 == 0 else 1
    outs, length = ([], extent // count)
    for k in range(count):
        piece = lax.slice_in_dim(value, k * length, (k + 1) * length, axis=dim)
        starts = jnp.arange(size) * extent + k * length
        outs.append(jax.vmap(apply)(lax.all_gather(piece, axis), starts))
    return in_order(jnp.concatenate(outs, axis=out_dim + 1), out_dim)


def in_blocks(value, dim, size):
    shape = value.shape
    tiles = value.reshape(*shape[:dim], size, shape[dim] // size, *shape[dim + 1 :])
    return jnp.moveaxis(tiles, dim, 0)


def sent_and_summed(value, axis, dim):
    tiles = in_blocks(value, dim, lax.axis_size(axis))
    arrived = lax.all_to_all(tiles, axis, split_axis=0, concat_axis=0, tiled=True)
    return arrived.astype(jnp.float32).sum(axis=0)


def normalize(summed):
    return lax.rsqrt(jnp.mean(summed * summed, axis=-1, keepdims=True) + epsilon)


def silu_slope(logits):
    sigmoid = jax.nn.sigmoid(logits)
    return sigmoid * (1.0 + logits * (1.0 - sigmoid))


def student_grads(
    start, injection, latents, pick_teacher, pick_depth, student_up, student_down, row_count
):
    previous = start
    records = []
    outputs = []
    for iteration in range(S_ITERS):
        summed = previous.astype(jnp.float32) + injection.astype(jnp.float32)
        factor = normalize(summed)
        normed = (summed * factor).astype(jnp.bfloat16)
        logits = jnp.dot(normed, student_up, preferred_element_type=jnp.float32)
        hidden = jax.nn.silu(logits).astype(jnp.bfloat16)
        previous = (
            previous.astype(jnp.float32)
            + jnp.dot(hidden, student_down, preferred_element_type=jnp.float32)
        ).astype(jnp.bfloat16)
        records.append((summed, factor, normed, logits, hidden))
        outputs.append(previous)
    target = start.astype(jnp.float32)
    iteration = 0
    target = jnp.where(
        pick_teacher[:, None] == iteration + 1, latents[iteration].astype(jnp.float32), target
    )
    result = jnp.zeros(start.shape, jnp.float32)
    for iteration in range(S_ITERS):
        result = jnp.where(
            pick_depth[:, None] == iteration + 1, outputs[iteration].astype(jnp.float32), result
        )
    slope = loss_scale * 2.0 / row_count * (result - target)
    grad_up = jnp.zeros(student_up.shape, jnp.float32)
    grad_down = jnp.zeros(student_down.shape, jnp.float32)
    carried = jnp.zeros(start.shape, jnp.float32)
    for iteration in reversed(range(S_ITERS)):
        summed, factor, normed, logits, hidden = records[iteration]
        cotangent = carried + jnp.where(pick_depth[:, None] == iteration + 1, slope, 0.0)
        rounded = cotangent.astype(jnp.bfloat16)
        grad_down = grad_down + jnp.dot(hidden.T, rounded, preferred_element_type=jnp.float32)
        upstream = jnp.dot(rounded, student_down.T, preferred_element_type=jnp.float32)
        local_grad = (upstream * silu_slope(logits)).astype(jnp.bfloat16)
        grad_up = grad_up + jnp.dot(normed.T, local_grad, preferred_element_type=jnp.float32)
        if iteration > 0:
            back_flow = jnp.dot(local_grad, student_up.T, preferred_element_type=jnp.float32)
            carried = (
                cotangent
                + factor * back_flow
                - summed * factor**3 * jnp.mean(summed * back_flow, axis=-1, keepdims=True)
            )
    return (grad_up, grad_down)


def body(
    teacher_state,
    injection,
    teacher_up,
    teacher_down,
    student_up,
    student_down,
    teacher_step,
    student_depth,
):
    slices = lax.axis_size("tp")
    group_rows = teacher_state.shape[0]
    own_count = group_rows // slices
    row_start = lax.axis_index("tp") * own_count

    def own_rows(whole):
        return lax.dynamic_slice_in_dim(whole, row_start, own_count, 0)

    latents = []
    summed = teacher_state.astype(jnp.float32) + injection.astype(jnp.float32)
    normed = (summed * normalize(summed)).astype(jnp.bfloat16)
    hidden = jax.nn.silu(jnp.dot(normed, teacher_up, preferred_element_type=jnp.float32)).astype(
        jnp.bfloat16
    )

    def columns(piece, start):
        return jnp.dot(hidden, piece, preferred_element_type=jnp.float32)

    row_share = lax.psum_scatter(
        on_gathered_pieces(teacher_down, "grp", 1, columns, 1).astype(jnp.bfloat16),
        "tp",
        scatter_dimension=0,
        tiled=True,
    ).astype(jnp.float32)
    row_state = (own_rows(teacher_state).astype(jnp.float32) + row_share).astype(jnp.bfloat16)
    latents.append(row_state)
    gathered_up, gathered_down = (
        lax.all_gather(student_up, "grp", axis=0, tiled=True),
        lax.all_gather(student_down, "grp", axis=1, tiled=True),
    )
    gathered_up, gathered_down = (
        lax.all_gather(gathered_up, "tp", axis=1, tiled=True),
        lax.all_gather(gathered_down, "tp", axis=0, tiled=True),
    )
    first_row = lax.axis_index("grp") * group_rows + row_start
    sequence = (first_row + jnp.arange(own_count, dtype=jnp.int32)) // LENGTH
    matches = sequence[:, None] == jnp.arange(teacher_step.shape[0], dtype=jnp.int32)[None, :]
    pick_teacher = jnp.sum(jnp.where(matches, teacher_step[None, :], 0), axis=1)
    pick_depth = jnp.sum(jnp.where(matches, student_depth[None, :], 0), axis=1)
    grad_up, grad_down = student_grads(
        own_rows(teacher_state),
        own_rows(injection),
        latents,
        pick_teacher,
        pick_depth,
        gathered_up,
        gathered_down,
        group_rows * lax.axis_size("grp"),
    )
    grad_up, grad_down = (
        lax.psum_scatter(
            grad_up.astype(jnp.bfloat16), "tp", scatter_dimension=1, tiled=True
        ).astype(jnp.float32),
        lax.psum_scatter(
            grad_down.astype(jnp.bfloat16), "tp", scatter_dimension=0, tiled=True
        ).astype(jnp.float32),
    )
    grad_up, grad_down = (
        sent_and_summed(grad_up.astype(jnp.bfloat16), "grp", 0),
        sent_and_summed(grad_down.astype(jnp.bfloat16), "grp", 1),
    )
    return (grad_up, grad_down)


def solution(mesh):
    in_specs = (
        P("grp", None),
        P("grp", None),
        P(None, "tp"),
        P("tp", "grp"),
        P("grp", "tp"),
        P("tp", "grp"),
        P(),
        P(),
    )
    out_specs = (P("grp", "tp"), P("tp", "grp"))
    return jax.shard_map(body, mesh=mesh, in_specs=in_specs, out_specs=out_specs, check_vma=False)
```

profile of v0, /device:TPU:0, one launch (start us, length us, event | category | flops | bytes accessed | tf_op | source)
XLA Modules:
  0.0 828.8 jit_solution(9276407297608392390)
XLA Ops:
  7.2 0.7 all-gather.12.cloned.1.call-update
  7.9 111.7 %all-gather.1 = bf16[32,165,64]{1,2,0:T(8,128)(2,1)S(1)} all-gather(bf16[1,165,64]{1,2,0:T(8,128)(2,1)} %bitcast.37), channel_id=1, replica_groups=mesh['tp'=4,'grp'=32] {'grp'}, dimensions={0}, use_global_device_ids=true | all-gather | bytes 696960 | tf_op jit(solution)/shard_map/all_gather | solution.py:137
  119.7 0.6 copy.27
  120.3 2.3 reshape.83
  122.6 103.0 %all-gather.2 = bf16[32,165,64]{1,2,0:T(8,128)(2,1)S(1)} all-gather(bf16[1,165,64]{1,2,0:T(8,128)(2,1)S(1)} %bitcast.38), channel_id=1, replica_groups=mesh['tp'=4,'grp'=32] {'grp'}, dimensions={0}, use_global_device_ids=true | all-gather | bytes 696960 | tf_op jit(solution)/shard_map/all_gather | solution.py:138
  225.6 1.6 copy.28
  227.1 3.1 reshape.85
  230.5 2.9 multiply_reduce_fusion
  233.4 13.2 %fusion.11 = bf16[256,2240,1]{0,1,2:T(8,128)(2,1)} fusion(bf16[5280,2240]{0,1:T(8,128)(2,1)} %param.10, bf16[256,5280]{0,1:T(8,128)(2,1)S(1)} %copy-done.8, bf16[256,5280]{0,1:T(8,128)(2,1)S(1)} %copy-done.10, f32[256]{0:T(256)S(1)} %add_rsqrt_fusion), kind=kOutput, calls=%fused_computation.22 | convolution fusion | flops 6065152000 | bytes 30209024 | tf_op jit(solution)/shard_map/dot_general | solution.py:121
  246.6 337.5 %all-gather.12.cloned.1.call-done = bf16[32,2240,165]{1,2,0:T(8,128)(2,1)} async-done(((bf16[1,2240,165]{1,2,0:T(8,128)(2,1)}), bf16[32,2240,165]{1,2,0:T(8,128)(2,1)}) %all-gather.12.cloned.1.call-update) | async-done | bytes 23654416 | tf_op jit(solution)/shard_map/all_gather | solution.py:25
  584.1 12.8 %convolution_convert_fusion = bf16[256,32,165]{0,2,1:T(8,128)(2,1)} fusion(bf16[256,2240,1]{0,1,2:T(8,128)(2,1)} %fusion.11, bf16[32,2240,165]{1,2,0:T(8,128)(2,1)} %all-gather.12.cloned.1.call-done), kind=kOutput, calls=%fused_computation.23 | convolution fusion | flops 6056878080 | bytes 27504640 | tf_op jit(solution)/shard_map/vmap()/dot_general | solution.py:126
  596.9 3.2 convert_element_type.106
  600.1 3.2 copy.29
  603.7 1.5 copy-done.9
  605.2 3.7 constant_dynamic-slice_fusion
  608.9 1.8 copy.33
  610.7 1.0 copy.32
  612.2 6.3 all-gather.8.cloned.1.call-done
  618.5 2.8 fusion.22
  621.2 28.7 %all-gather.10.cloned.1.call-done = bf16[256,5280]{1,0:T(8,128)(2,1)} async-done(((bf16[64,5280]{1,0:T(8,128)(2,1)}), bf16[256,5280]{1,0:T(8,128)(2,1)}) %all-gather.10.cloned.1.call-update) | async-done | bytes 2703376 | tf_op jit(solution)/shard_map/all_gather | solution.py:142
  649.9 2.5 multiply_reduce_fusion.2
  652.4 0.5 multiply_multiply_fusion
  652.9 0.6 copy-done.1
  653.7 0.9 copy-done.6
  654.7 1.6 fusion.23
  656.3 37.9 %reduce-scatter.4.cloned.1.call-done = bf16[64,5280]{1,0:T(8,128)(2,1)} async-done(((bf16[256,5280]{1,0:T(8,128)(2,1)}), bf16[64,5280]{1,0:T(8,128)(2,1)}) %reduce-scatter.4.cloned.1.call-update) | async-done | bytes 675856 | tf_op jit(solution)/shard_map/reduce_scatter | solution.py:128
  694.1 2.5 fusion.8
  696.6 0.9 fusion.21
  697.6 1.0 fusion.13
  698.6 0.3 copy-done.2
  698.9 0.9 copy-done.4
  699.8 0.8 multiply_reduce_fusion.1
  700.5 0.6 add_convert_fusion
  701.1 0.9 copy-done.7
  702.0 2.5 fusion.1
  704.8 4.4 fusion.24
  709.2 7.8 fusion
  717.0 29.3 %reduce-scatter.8.cloned.1.call-done = bf16[64,5280]{1,0:T(8,128)(2,1)} async-done(((bf16[256,5280]{1,0:T(8,128)(2,1)}), bf16[64,5280]{1,0:T(8,128)(2,1)}) %reduce-scatter.8.cloned.1.call-update) | async-done | bytes 675856 | tf_op jit(solution)/shard_map/reduce_scatter | solution.py:163
  746.3 4.1 reshape.80
  750.4 1.6 copy.35
  752.0 7.2 all-to-all-start.1
  759.2 31.8 %reduce-scatter.6.cloned.1.call-done = bf16[5280,64]{0,1:T(8,128)(2,1)} async-done(((bf16[5280,256]{0,1:T(8,128)(2,1)}), bf16[5280,64]{0,1:T(8,128)(2,1)}) %reduce-scatter.6.cloned.1.call-update) | async-done | bytes 675856 | tf_op jit(solution)/shard_map/reduce_scatter | solution.py:160
  791.0 4.1 reshape.79
  795.1 1.6 copy.30
  796.7 6.8 all-to-all-start
  803.5 0.8 convert_reduce_fusion
  804.3 16.9 %all-to-all-done = bf16[32,165,64]{1,2,0:T(8,128)(2,1)S(1)} async-done(((bf16[32,165,64]{1,2,0:T(8,128)(2,1)}), bf16[32,165,64]{1,2,0:T(8,128)(2,1)S(1)}, u32[]{:S(2)}, u32[]{:S(2)}) %all-to-all-start) | async-done | bytes 675872 | tf_op jit(solution)/shard_map/all_to_all | solution.py:37
  821.2 0.8 convert_reduce_fusion.1
  (48 shorter events, 1.8 us)
Async XLA Ops:
  7.2 576.9 %all-gather.12.cloned.1.call-start = ((), (), s32[]{:S(2)}) async-start(), calls=%async_computation.10 | async-start | bytes 25546752 | tf_op jit(solution)/shard_map/all_gather | solution.py:25
  7.9 610.6 %all-gather.8.cloned.1.call-start = ((), (), s32[]{:S(2)}) async-start(), calls=%async_computation.5 | async-start | bytes 3440640 | tf_op jit(solution)/shard_map/all_gather | solution.py:141
  119.7 2.9 copy-start.13
  122.6 527.4 %all-gather.10.cloned.1.call-start = ((), (), s32[]{:S(2)}) async-start(), calls=%async_computation.6 | async-start | bytes 3440640 | tf_op jit(solution)/shard_map/all_gather | solution.py:142
  225.6 4.9 copy-start.8
  230.2 463.9 %reduce-scatter.4.cloned.1.call-start = ((), (), s32[]{:S(2)}) async-start(), calls=%async_computation.7 | async-start | bytes 3440640 | tf_op jit(solution)/shard_map/reduce_scatter | solution.py:128
  230.5 2.9 copy-start.10
  603.4 1.8 copy-start.9
  603.4 142.9 %reduce-scatter.8.cloned.1.call-start = ((), (), s32[]{:S(2)}) async-start(), calls=%async_computation.9 | async-start | bytes 3440640 | tf_op jit(solution)/shard_map/reduce_scatter | solution.py:163
  608.9 1.8 copy-start.11
  608.9 2.9 copy-start.14
  608.9 2.9 copy-start.15
  611.7 38.2 %copy-start.5 = (bf16[64,5280]{1,0:T(8,128)(2,1)}, bf16[64,5280]{1,0:T(8,128)(2,1)S(1)}, u32[]{:S(2)}) copy-start(bf16[64,5280]{1,0:T(8,128)(2,1)S(1)} %copy.32) | copy-start | bytes 2027524
  652.4 1.1 copy-start.1
  652.4 2.3 copy-start.3
  653.7 0.9 copy-start.6
  654.7 39.5 %copy-start = (bf16[256,5280]{1,0:T(8,128)(2,1)S(1)}, bf16[256,5280]{1,0:T(8,128)(2,1)}, u32[]{:S(2)}) copy-start(bf16[256,5280]{1,0:T(8,128)(2,1)} %all-gather.10.cloned.1.call-done) | copy-start | bytes 8110084
  694.1 2.5 copy-start.12
  697.5 1.3 copy-start.2
  697.6 2.2 copy-start.4
  699.8 0.8 copy-start.16
  701.1 0.9 copy-start.7
  704.5 86.5 %reduce-scatter.6.cloned.1.call-start = ((), (), s32[]{:S(2)}) async-start(), calls=%async_computation.8 | async-start | bytes 3440640 | tf_op jit(solution)/shard_map/reduce_scatter | solution.py:160
  752.0 44.7 %all-to-all-start.1 = ((bf16[32,64,165]{2,1,0:T(8,128)(2,1)}), bf16[32,64,165]{2,1,0:T(8,128)(2,1)S(1)}, u32[]{:S(2)}, u32[]{:S(2)}) async-start(bf16[32,64,165]{2,1,0:T(8,128)(2,1)} %bitcast.34), calls=%async_computation.4 | async-start | bytes 2097152 | tf_op jit(solution)/shard_map/all_to_all | solution.py:37
  796.7 24.5 %all-to-all-start = ((bf16[32,165,64]{1,2,0:T(8,128)(2,1)}), bf16[32,165,64]{1,2,0:T(8,128)(2,1)S(1)}, u32[]{:S(2)}, u32[]{:S(2)}) async-start(bf16[32,165,64]{1,2,0:T(8,128)(2,1)} %copy.30), calls=%async_computation.2 | async-start | bytes 2097152 | tf_op jit(solution)/shard_map/all_to_all | solution.py:37
Sparse Core Ops, SparseCore 0:
  9.6 574.4 all-gather.11
  585.7 32.6 all-gather.7
  620.1 29.7 all-gather.9
  652.4 41.6 reduce-scatter.3
  704.6 41.6 reduce-scatter.7
  748.8 42.1 reduce-scatter.5
where the time goes:
time: 830 us; the launch traced here: 829 us
  waiting for transfers between devices  489 us (59%)
  blocking collectives  215 us (26%)
  matrix products  52.7 us (6%)
  local copies, waits for them, and re-layouts  36.8 us (4%)
  starting transfers between devices  14.9 us (2%)
  between operations  14.4 us (2%)
    all_gather x1, waiting for transfers between devices, on_gathered_pieces(): outs.append(jax.vmap(apply)(lax.all_gather(piece, axis), starts))  338 us
    all_gather x1, blocking collectives, body(): lax.all_gather(student_up, 'grp', axis=0, tiled=True)  112 us
    all_gather x1, blocking collectives, body(): lax.all_gather(student_down, 'grp', axis=1, tiled=True)  103 us
    reduce_scatter x1, waiting for transfers between devices, body(): lax.psum_scatter(on_gathered_pieces(teacher_down, 'grp', 1, columns, 1).a...  37.9 us
    reduce_scatter x1, waiting for transfers between devices, body(): lax.psum_scatter(grad_up.astype(jnp.bfloat16), 'tp', scatter_dimension=1,...  31.8 us
    reduce_scatter x1, waiting for transfers between devices, body(): lax.psum_scatter(grad_down.astype(jnp.bfloat16), 'tp', scatter_dimension=...  29.3 us
    all_gather x1, waiting for transfers between devices, body(): lax.all_gather(gathered_down, 'tp', axis=0, tiled=True)  28.7 us
    all_to_all x2, waiting for transfers between devices, sent_and_summed(): lax.all_to_all(tiles, axis, split_axis=0, concat_axis=0, tiled=True)  16.9 us
  transfers between devices with their start and end apart: 8, of which 7 were waited for; matrix products, arithmetic and copies ran while one was open for 10% of the time, Pallas kernels for 0%

commit v1 on v0

--- a/solution.py
+++ b/solution.py
@@ -7,6 +7,11 @@
 S_ITERS = 2
 epsilon = 1e-06
 loss_scale = 64.0
+
+
+def update_spot(array_in):
+    response = jnp.concatenate(lax.all_gather(array_in, "grp"), 1)
+    return response
 
 
 def in_order(tiles, dim):
@@ -135,7 +140,7 @@
     latents.append(row_state)
     gathered_up, gathered_down = (
         lax.all_gather(student_up, "grp", axis=0, tiled=True),
-        lax.all_gather(student_down, "grp", axis=1, tiled=True),
+        update_spot(student_down),
     )
     gathered_up, gathered_down = (
         lax.all_gather(gathered_up, "tp", axis=1, tiled=True),

time: 830 us -> 830 us (level)
  no operation moved by 1% of the time
where the time goes in v1:
time: 830 us; the launch traced here: 829 us
  waiting for transfers between devices  489 us (59%)
  blocking collectives  215 us (26%)
  matrix products  52.7 us (6%)
  local copies, waits for them, and re-layouts  36.8 us (4%)
  starting transfers between devices  14.9 us (2%)
  between operations  14.4 us (2%)
    all_gather x1, waiting for transfers between devices, on_gathered_pieces(): outs.append(jax.vmap(apply)(lax.all_gather(piece, axis), starts))  338 us
    all_gather x1, blocking collectives, body(): lax.all_gather(student_up, 'grp', axis=0, tiled=True)  112 us
    all_gather x1, blocking collectives, update_spot(): response = jnp.concatenate(lax.all_gather(array_in, 'grp'), 1)  103 us
    reduce_scatter x1, waiting for transfers between devices, body(): lax.psum_scatter(on_gathered_pieces(teacher_down, 'grp', 1, columns, 1).a...  37.9 us
    reduce_scatter x1, waiting for transfers between devices, body(): lax.psum_scatter(grad_up.astype(jnp.bfloat16), 'tp', scatter_dimension=1,...  31.8 us
    reduce_scatter x1, waiting for transfers between devices, body(): lax.psum_scatter(grad_down.astype(jnp.bfloat16), 'tp', scatter_dimension=...  29.3 us
    all_gather x1, waiting for transfers between devices, body(): lax.all_gather(gathered_down, 'tp', axis=0, tiled=True)  28.7 us
    all_to_all x2, waiting for transfers between devices, sent_and_summed(): lax.all_to_all(tiles, axis, split_axis=0, concat_axis=0, tiled=True)  16.9 us
  transfers between devices with their start and end apart: 8, of which 7 were waited for; matrix products, arithmetic and copies ran while one was open for 10% of the time, Pallas kernels for 0%

profile of v1, /device:TPU:0, one launch (start us, length us, event | category | flops | bytes accessed | tf_op | source)
XLA Modules:
  0.0 828.8 jit_solution(11721976496536972455)
XLA Ops:
  7.2 0.7 all-gather.12.cloned.1.call-update
  7.9 111.7 %all-gather.2 = bf16[32,165,64]{1,2,0:T(8,128)(2,1)S(1)} all-gather(bf16[1,165,64]{1,2,0:T(8,128)(2,1)} %bitcast.36), channel_id=1, replica_groups=mesh['tp'=4,'grp'=32] {'grp'}, dimensions={0}, use_global_device_ids=true | all-gather | bytes 696960 | tf_op jit(solution)/shard_map/all_gather | solution.py:142
  119.7 0.6 copy.27
  120.3 2.3 reshape.92
  122.6 103.0 %all-gather = bf16[2048,165]{1,0:T(8,128)(2,1)S(1)} all-gather(bf16[64,165]{1,0:T(8,128)(2,1)S(1)} %copy-done.13), channel_id=2, replica_groups=mesh['tp'=4,'grp'=32] {'grp'}, dimensions={0}, use_global_device_ids=true | all-gather | bytes 696960 | tf_op jit(solution)/shard_map/all_gather | solution.py:13
  225.6 1.6 copy.37
  227.1 3.1 reshape.86
  230.5 2.9 multiply_reduce_fusion
  233.4 13.2 %fusion.11 = bf16[256,2240,1]{0,1,2:T(8,128)(2,1)} fusion(bf16[5280,2240]{0,1:T(8,128)(2,1)} %param.10, bf16[256,5280]{0,1:T(8,128)(2,1)S(1)} %copy-done.8, bf16[256,5280]{0,1:T(8,128)(2,1)S(1)} %copy-done.10, f32[256]{0:T(256)S(1)} %add_rsqrt_fusion), kind=kOutput, calls=%fused_computation.22 | convolution fusion | flops 6065152000 | bytes 30209024 | tf_op jit(solution)/shard_map/dot_general | solution.py:126
  246.6 337.5 %all-gather.12.cloned.1.call-done = bf16[32,2240,165]{1,2,0:T(8,128)(2,1)} async-done(((bf16[1,2240,165]{1,2,0:T(8,128)(2,1)}), bf16[32,2240,165]{1,2,0:T(8,128)(2,1)}) %all-gather.12.cloned.1.call-update) | async-done | bytes 23654416 | tf_op jit(solution)/shard_map/all_gather | solution.py:30
  584.1 12.8 %convolution_convert_fusion = bf16[256,32,165]{0,2,1:T(8,128)(2,1)} fusion(bf16[256,2240,1]{0,1,2:T(8,128)(2,1)} %fusion.11, bf16[32,2240,165]{1,2,0:T(8,128)(2,1)} %all-gather.12.cloned.1.call-done), kind=kOutput, calls=%fused_computation.23 | convolution fusion | flops 6056878080 | bytes 27504640 | tf_op jit(solution)/shard_map/vmap()/dot_general | solution.py:131
  596.9 3.2 convert_element_type.106
  600.1 3.2 copy.29
  603.7 1.5 copy-done.9
  605.2 3.7 constant_dynamic-slice_fusion
  608.9 1.8 copy.33
  610.7 1.0 copy.32
  612.2 6.3 all-gather.8.cloned.1.call-done
  618.5 2.8 fusion.22
  621.2 28.7 %all-gather.10.cloned.1.call-done = bf16[256,5280]{1,0:T(8,128)(2,1)} async-done(((bf16[64,5280]{1,0:T(8,128)(2,1)}), bf16[256,5280]{1,0:T(8,128)(2,1)}) %all-gather.10.cloned.1.call-update) | async-done | bytes 2703376 | tf_op jit(solution)/shard_map/all_gather | solution.py:147
  649.9 2.5 multiply_reduce_fusion.2
  652.4 0.5 multiply_multiply_fusion
  652.9 0.6 copy-done.1
  653.7 0.9 copy-done.6
  654.7 1.6 fusion.23
  656.3 37.9 %reduce-scatter.4.cloned.1.call-done = bf16[64,5280]{1,0:T(8,128)(2,1)} async-done(((bf16[256,5280]{1,0:T(8,128)(2,1)}), bf16[64,5280]{1,0:T(8,128)(2,1)}) %reduce-scatter.4.cloned.1.call-update) | async-done | bytes 675856 | tf_op jit(solution)/shard_map/reduce_scatter | solution.py:133
  694.1 2.5 fusion.8
  696.6 0.9 fusion.21
  697.6 1.0 fusion.13
  698.6 0.3 copy-done.2
  698.9 0.9 copy-done.4
  699.8 0.8 multiply_reduce_fusion.1
  700.5 0.6 add_convert_fusion
  701.1 0.9 copy-done.7
  702.0 2.5 fusion.1
  704.8 4.4 fusion.24
  709.2 7.8 fusion
  717.0 29.3 %reduce-scatter.8.cloned.1.call-done = bf16[64,5280]{1,0:T(8,128)(2,1)} async-done(((bf16[256,5280]{1,0:T(8,128)(2,1)}), bf16[64,5280]{1,0:T(8,128)(2,1)}) %reduce-scatter.8.cloned.1.call-update) | async-done | bytes 675856 | tf_op jit(solution)/shard_map/reduce_scatter | solution.py:168
  746.3 4.1 reshape.88
  750.4 1.6 copy.36
  752.0 7.2 all-to-all-start.1
  759.2 31.8 %reduce-scatter.6.cloned.1.call-done = bf16[5280,64]{0,1:T(8,128)(2,1)} async-done(((bf16[5280,256]{0,1:T(8,128)(2,1)}), bf16[5280,64]{0,1:T(8,128)(2,1)}) %reduce-scatter.6.cloned.1.call-update) | async-done | bytes 675856 | tf_op jit(solution)/shard_map/reduce_scatter | solution.py:165
  791.0 4.1 reshape.87
  795.1 1.6 copy.30
  796.7 6.8 all-to-all-start
  803.5 0.8 convert_reduce_fusion
  804.3 16.9 %all-to-all-done = bf16[32,165,64]{1,2,0:T(8,128)(2,1)S(1)} async-done(((bf16[32,165,64]{1,2,0:T(8,128)(2,1)}), bf16[32,165,64]{1,2,0:T(8,128)(2,1)S(1)}, u32[]{:S(2)}, u32[]{:S(2)}) %all-to-all-start) | async-done | bytes 675872 | tf_op jit(solution)/shard_map/all_to_all | solution.py:42
  821.2 0.8 convert_reduce_fusion.1
  (48 shorter events, 1.8 us)
Async XLA Ops:
  7.2 576.9 %all-gather.12.cloned.1.call-start = ((), (), s32[]{:S(2)}) async-start(), calls=%async_computation.10 | async-start | bytes 25546752 | tf_op jit(solution)/shard_map/all_gather | solution.py:30
  7.9 610.6 %all-gather.8.cloned.1.call-start = ((), (), s32[]{:S(2)}) async-start(), calls=%async_computation.5 | async-start | bytes 3440640 | tf_op jit(solution)/shard_map/all_gather | solution.py:146
  119.7 2.9 copy-start.13
  122.6 527.4 %all-gather.10.cloned.1.call-start = ((), (), s32[]{:S(2)}) async-start(), calls=%async_computation.6 | async-start | bytes 3440640 | tf_op jit(solution)/shard_map/all_gather | solution.py:147
  225.6 4.9 copy-start.8
  230.2 463.9 %reduce-scatter.4.cloned.1.call-start = ((), (), s32[]{:S(2)}) async-start(), calls=%async_computation.7 | async-start | bytes 3440640 | tf_op jit(solution)/shard_map/reduce_scatter | solution.py:133
  230.5 2.9 copy-start.10
  603.4 1.8 copy-start.9
  603.4 142.9 %reduce-scatter.8.cloned.1.call-start = ((), (), s32[]{:S(2)}) async-start(), calls=%async_computation.9 | async-start | bytes 3440640 | tf_op jit(solution)/shard_map/reduce_scatter | solution.py:168
  608.9 1.8 copy-start.11
  608.9 2.9 copy-start.14
  608.9 2.9 copy-start.15
  611.7 38.2 %copy-start.5 = (bf16[64,5280]{1,0:T(8,128)(2,1)}, bf16[64,5280]{1,0:T(8,128)(2,1)S(1)}, u32[]{:S(2)}) copy-start(bf16[64,5280]{1,0:T(8,128)(2,1)S(1)} %copy.32) | copy-start | bytes 2027524
  652.4 1.1 copy-start.1
  652.4 2.3 copy-start.3
  653.7 0.9 copy-start.6
  654.7 39.5 %copy-start = (bf16[256,5280]{1,0:T(8,128)(2,1)S(1)}, bf16[256,5280]{1,0:T(8,128)(2,1)}, u32[]{:S(2)}) copy-start(bf16[256,5280]{1,0:T(8,128)(2,1)} %all-gather.10.cloned.1.call-done) | copy-start | bytes 8110084
  694.1 2.5 copy-start.12
  697.5 1.3 copy-start.2
  697.6 2.2 copy-start.4
  699.8 0.8 copy-start.16
  701.1 0.9 copy-start.7
  704.5 86.5 %reduce-scatter.6.cloned.1.call-start = ((), (), s32[]{:S(2)}) async-start(), calls=%async_computation.8 | async-start | bytes 3440640 | tf_op jit(solution)/shard_map/reduce_scatter | solution.py:165
  752.0 44.7 %all-to-all-start.1 = ((bf16[32,64,165]{2,1,0:T(8,128)(2,1)}), bf16[32,64,165]{2,1,0:T(8,128)(2,1)S(1)}, u32[]{:S(2)}, u32[]{:S(2)}) async-start(bf16[32,64,165]{2,1,0:T(8,128)(2,1)} %bitcast.31), calls=%async_computation.4 | async-start | bytes 2097152 | tf_op jit(solution)/shard_map/all_to_all | solution.py:42
  796.7 24.5 %all-to-all-start = ((bf16[32,165,64]{1,2,0:T(8,128)(2,1)}), bf16[32,165,64]{1,2,0:T(8,128)(2,1)S(1)}, u32[]{:S(2)}, u32[]{:S(2)}) async-start(bf16[32,165,64]{1,2,0:T(8,128)(2,1)} %copy.30), calls=%async_computation.2 | async-start | bytes 2097152 | tf_op jit(solution)/shard_map/all_to_all | solution.py:42
Sparse Core Ops, SparseCore 0:
  9.6 574.4 all-gather.11
  585.7 32.6 all-gather.7
  620.1 29.7 all-gather.9
  652.4 41.6 reduce-scatter.3
  704.6 41.6 reduce-scatter.7
  748.8 42.1 reduce-scatter.5
